TPU v7x, 128 devices: a whole 4x4x4 slice. The times are simulated.
128 devices in a mesh: ops: 16 (over z, x_hi, core), blk: 8 (over y, x_lo).
Axes of the slice: x: 4 (x_hi: 2, x_lo: 2; x = x_hi * 2 + x_lo), y: 4, z: 4, core: 2. Of those that a mesh axis runs over, the one named last changes fastest.
Arguments:
- psi: bfloat16 [2048, 1024], P('blk'), may hold values from -6 to 6
- left_blocks: bfloat16 [256, 16, 128, 128], P('ops', 'blk'), may hold values from -0.5 to 0.5
- right_ops: bfloat16 [256, 1024, 1024], P(('ops', 'blk')), may hold values from -0.046875 to 0.046875
- block_target: int32 [256, 16], P('ops'), may hold values from 0 to 15
- left_partner: int32 [256], P('ops'), may hold values from 0 to 255, as said below
- block_len: int32 [16], replicated, may hold values from 1 to 128, 1536 in all
Outputs:
- sigma: bfloat16 [2048, 1024], P('blk', 'ops')
Inputs may be any that keep to these rules, and one draw needn't show every extreme that they name: left_partner is a permutation of 0 to 255 that maps each aligned group of 16 operators onto itself.
All inputs are finite; a program needn't handle non-finite values.
Results may differ from a plain program's by a relative error of at most 0.018.
Values may be sent and summed in bfloat16 or wider, within the bound.
A program may use at most 128 MiB of HBM per device.

v0:
```python
import jax
import jax.numpy as jnp
from jax import lax
from jax.sharding import PartitionSpec as P


def split_up(shard, dim, size):
    shape = shard.shape
    tiles = shard.reshape(*shape[:dim], size, shape[dim] // size, *shape[dim + 1 :])
    return jnp.moveaxis(tiles, dim, 0)


def sent_and_summed(shard, axis, dim):
    tiles = split_up(shard, dim, lax.axis_size(axis))
    arrived = lax.all_to_all(tiles, axis, split_axis=0, concat_axis=0, tiled=True)
    return arrived.astype(jnp.float32).sum(axis=0)


def add_blocks(running, mixed, targets):
    for source in range(mixed.shape[0]):
        where = targets[source]
        current = lax.dynamic_index_in_dim(running, where, 0, keepdims=False)
        running = lax.dynamic_update_index_in_dim(running, current + mixed[source], where, 0)
    return running


def local(psi, left_blocks, right_ops, block_target, left_partner, block_len):
    group_size = left_blocks.shape[0]
    local_blocks = left_blocks.shape[1]
    block_rows = left_blocks.shape[2]
    columns = psi.shape[1]
    blocks_all = block_target.shape[1]
    column_index = lax.axis_index("blk")
    group_index = lax.axis_index("ops")
    first_op = group_index * group_size
    row_index = jnp.arange(block_rows, dtype=jnp.int32)
    live_rows = row_index[None, :] < block_len[:, None]
    live_local = lax.dynamic_slice_in_dim(live_rows, column_index * local_blocks, local_blocks, 0)
    states = psi.reshape(local_blocks, block_rows, columns) * live_local[:, :, None].astype(
        jnp.bfloat16
    )
    blank = jnp.zeros((blocks_all, block_rows, columns), jnp.float32)
    all_states, all_blocks = (
        lax.all_gather(states, "blk", axis=0, tiled=True),
        lax.all_gather(left_blocks, "blk", axis=1, tiled=True),
    )
    stacked = all_states.reshape(blocks_all * block_rows, columns)
    local_ops = right_ops.shape[0]

    def apply_own(step, running):
        image = jnp.dot(stacked, right_ops[step], preferred_element_type=jnp.float32).astype(
            jnp.bfloat16
        )
        image = image.reshape(blocks_all, block_rows, columns)
        owner = left_partner[column_index * local_ops + step] - first_op
        mixed = jnp.einsum(
            "qab,qbr->qar", all_blocks[owner], image, preferred_element_type=jnp.float32
        )
        return add_blocks(running, mixed, block_target[owner])

    partial_sum = lax.fori_loop(0, local_ops, apply_own, blank)
    flat_sum = partial_sum.reshape(blocks_all * block_rows, columns)
    owned = lax.psum_scatter(
        flat_sum.astype(jnp.bfloat16), "ops", scatter_dimension=1, tiled=True
    ).astype(jnp.float32)
    owned = sent_and_summed(owned.astype(jnp.bfloat16), "blk", 0)
    result = owned.reshape(local_blocks, block_rows, -1) * live_local[:, :, None].astype(
        jnp.float32
    )
    return result.reshape(local_blocks * block_rows, -1).astype(jnp.bfloat16)


def solution(mesh):
    return jax.shard_map(
        local,
        mesh=mesh,
        in_specs=(
            P("blk", None),
            P("ops", "blk", None, None),
            P(("ops", "blk"), None, None),
            P("ops", None),
            P("ops"),
            P(),
        ),
        out_specs=P("blk", "ops"),
        check_vma=False,
    )
```

profile of v0, /device:TPU:1, one launch (start us, length us, event | category | flops | bytes accessed | tf_op | source)
XLA Modules:
  0.0 555.2 jit_solution(6440675355130429110)
XLA Ops:
  7.4 2.0 broadcast_multiply_fusion
  10.2 92.8 %all-gather.5.cloned.1.call-done = bf16[16,128,1024]{2,1,0:T(8,128)(2,1)} async-done(((bf16[2,128,1024]{2,1,0:T(8,128)(2,1)}), bf16[16,128,1024]{2,1,0:T(8,128)(2,1)}) %all-gather.5.cloned.1.call-update) | async-done | bytes 4194320 | tf_op jit(solution)/shard_map/all_gather | solution.py:44
  103.0 170.1 %all-gather.3.cloned.1.call-done = bf16[16,16,128,128]{3,2,1,0:T(8,128)(2,1)} async-done(((bf16[16,2,128,128]{3,2,1,0:T(8,128)(2,1)}), bf16[16,16,128,128]{3,2,1,0:T(8,128)(2,1)}) %all-gather.3.cloned.1.call-update) | async-done | bytes 8388624 | tf_op jit(solution)/shard_map/all_gather | solution.py:45
  273.1 4.3 broadcast_in_dim.56
  277.4 166.0 %while.15 = (s32[]{:T(128)}, f32[16,128,1024]{2,1,0:T(8,128)}, s32[]{:T(128)}, s32[16]{0:T(128)S(1)}, s32[]{:T(128)}, /*index=5*/s32[16,16]{1,0:T(8,128)}, bf16[...) while((s32[]{:T(128)}, f32[16,128,1024]{2,1,0:T(8,128)}, ...), condition=%wide.region_1.2_spmd, body=%wide.region_0.1_spmd.sunk | while | flops 4836032512 | bytes 57148468 | solution.py:61
  310.2 9.4 %convert_bitcast_fusion.2 = bf16[2048,1024]{0,1:T(8,128)(2,1)} fusion(bf16[2048,1024]{1,0:T(8,128)(2,1)} %get-tuple-element.373, bf16[2,1024,1024]{2,1,0:T(8,128)(2,1)} %get-tuple-element.372, s32[]{:T(128)S(6)} %copy.40), kind=kOutput, calls=%fused_computation.clone.1 | convolution fusion | flops 4297064448 | bytes 10485764 | tf_op jit(solution)/shard_map/while/body/eval_jaxpr/dot_general | solution.py:51
  319.6 6.4 %copy.21 = bf16[2048,1024]{1,0:T(8,128)(2,1)} copy(bf16[2048,1024]{0,1:T(8,128)(2,1)} %convert_bitcast_fusion.2) | data formatting | bytes 8388608 | tf_op jit(solution)/shard_map/while/body/eval_jaxpr/reshape | solution.py:54
  326.0 3.6 fusion.56
  331.5 1.9 fusion.58
  339.2 1.9 fusion.62
  343.1 2.0 fusion.64
  346.9 2.0 fusion.66
  354.6 2.0 fusion.70
  358.5 1.9 fusion.72
  393.2 9.4 %convert_bitcast_fusion.2 = bf16[2048,1024]{0,1:T(8,128)(2,1)} fusion(bf16[2048,1024]{1,0:T(8,128)(2,1)} %get-tuple-element.373, bf16[2,1024,1024]{2,1,0:T(8,128)(2,1)} %get-tuple-element.372, s32[]{:T(128)S(6)} %copy.40), kind=kOutput, calls=%fused_computation.clone.1 | convolution fusion | flops 4297064448 | bytes 10485764 | tf_op jit(solution)/shard_map/while/body/eval_jaxpr/dot_general | solution.py:51
  402.6 6.4 %copy.21 = bf16[2048,1024]{1,0:T(8,128)(2,1)} copy(bf16[2048,1024]{0,1:T(8,128)(2,1)} %convert_bitcast_fusion.2) | data formatting | bytes 8388608 | tf_op jit(solution)/shard_map/while/body/eval_jaxpr/reshape | solution.py:54
  409.0 3.6 fusion.56
  416.5 1.9 fusion.59
  418.4 1.9 fusion.60
  422.2 1.9 fusion.62
  443.4 6.0 %convert_element_type.33 = bf16[16,128,1024]{2,1,0:T(8,128)(2,1)} convert(f32[16,128,1024]{2,1,0:T(8,128)} %get-tuple-element.217) | non-fusion elementwise | flops 2097152 | bytes 12582912 | tf_op jit(solution)/shard_map/convert_element_type | solution.py:64
  449.4 6.5 %copy.17 = bf16[2048,1024]{0,1:T(8,128)(2,1)} copy(bf16[2048,1024]{1,0:T(8,128)(2,1)} %bitcast.83) | data formatting | bytes 8388608
  455.9 80.7 %reduce-scatter.4.cloned.1.call-done = bf16[64,2048]{1,0:T(8,128)(2,1)} async-done(((bf16[1024,2048]{1,0:T(8,128)(2,1)}), bf16[64,2048]{1,0:T(8,128)(2,1)}) %reduce-scatter.4.cloned.1.call-update) | async-done | bytes 262160
  538.1 9.9 %all_to_all.5 = bf16[8,256,64]{1,2,0:T(8,128)(2,1)S(1)} all-to-all(bf16[8,256,64]{1,2,0:T(8,128)(2,1)S(1)} %copy.13), channel_id=1, replica_groups=mesh['ops'=16,'blk'=8] {'blk'}, dimensions={0} | all-to-all | bytes 524288 | tf_op jit(solution)/shard_map/all_to_all | solution.py:15
  (43 shorter events, 51.8 us)
Async XLA Ops:
  6.5 270.9 %copy-start = (s32[16]{0:T(128)S(1)}, s32[16]{0:T(128)}, u32[]{:S(2)}) copy-start(s32[16]{0:T(128)} %param.12) | copy-start | bytes 196
  6.5 96.5 %all-gather.5.cloned.1.call-start = ((), (), s32[]{:S(2)}) async-start(), calls=%async_computation.3 | async-start | bytes 4718592 | tf_op jit(solution)/shard_map/all_gather | solution.py:44
  9.4 263.8 %all-gather.3.cloned.1.call-start = ((), (), s32[]{:S(2)}) async-start(), calls=%async_computation.2 | async-start | bytes 9437184 | tf_op jit(solution)/shard_map/all_gather | solution.py:45
  10.1 526.5 %reduce-scatter.4.cloned.1.call-start = ((), (), s32[]{:S(2)}) async-start(), calls=%async_computation.4 | async-start | bytes 4456448
Sparse Core Ops, SparseCore 0:
  9.5 93.4 all-gather.4
  104.6 168.4 all-gather.2
  456.1 80.5 reduce-scatter.3
where the time goes:
time: 561 us; the launch traced here: 555 us
  waiting for transfers between devices  344 us (61%)
  other arithmetic  70.4 us (13%)
  loops' own time  61.6 us (11%)
  local copies, waits for them, and re-layouts  29.7 us (5%)
  matrix products  25.9 us (5%)
  between operations  13.1 us (2%)
  blocking collectives  9.94 us (2%)
    all_gather x1, waiting for transfers between devices, local(): lax.all_gather(left_blocks, 'blk', axis=1, tiled=True)  170 us
    all_gather x1, waiting for transfers between devices, local(): lax.all_gather(states, 'blk', axis=0, tiled=True)  92.8 us
    unnamed x4, waiting for transfers between devices  81.4 us
    dynamic_update_slice x32, other arithmetic, add_blocks(): lax.dynamic_update_index_in_dim(running, current + mixed[source], where, 0)  61.7 us
    another operation x1, loops' own time, local(): partial_sum = lax.fori_loop(0, local_ops, apply_own, blank)  61.6 us
    dot_general x2, matrix products, apply_own(): jnp.dot(stacked, right_ops[step], preferred_element_type=jnp.float32)  18.7 us
    reshape x2, local copies, waits for them, and re-layouts, apply_own(): image = image.reshape(blocks_all, block_rows, columns)  12.8 us
  transfers between devices with their start and end apart: 3, of which 3 were waited for; matrix products, arithmetic and copies ran while one was open for 0% of the time, Pallas kernels for 0%

commit v1 on v0

v1 whole, which is shorter than its diff:
```python
import jax
import jax.numpy as jnp
from jax import lax
from jax.experimental import pallas as pl
from jax.experimental.pallas import tpu as pltpu
from jax.sharding import PartitionSpec as P

MESH = pl.DeviceIdType.MESH
F32, BF16 = jnp.float32, jnp.bfloat16
VMEM, SMEM, DMA = pltpu.VMEM, pltpu.SMEM, pltpu.SemaphoreType.DMA
PZ, PX, PY = 48, 48, 32


def order_kernel(partner, targets, table, fill):
    blk = lax.axis_index("blk")
    owners = [lax.rem(partner[blk * 2 + i], 16) for i in range(2)]
    for t in range(16):
        fill[t] = 0

    @pl.loop(0, 8)
    def _(c):
        for i in range(2):
            for e in range(2):
                t = targets[owners[i], 2 * c + e]
                fill[t] = fill[t] + 1

    begin = jnp.int32(0)
    for t in range(16):
        count = fill[t]
        fill[t] = begin
        table[80 + t] = begin
        table[96 + t] = jnp.where(count > 0, 1, 0)
        begin = begin + count
        table[64 + t] = jnp.maximum(begin - 1, 0)

    @pl.loop(0, 8)
    def _(c):
        for i in range(2):
            for e in range(2):
                t = targets[owners[i], 2 * c + e]
                at = fill[t]
                table[at] = c * 4 + i * 2 + e
                table[32 + at] = jnp.where(at > table[80 + t], 1, 0)
                fill[t] = at + 1


def kernel(
    partner, lens, table, psi, left, right, out,
    states, lsend, lrecv, lin, rops, image, runs, dsend, drecv,
    s1z, s1x, s1y, r1z, r1x, r1y, s2z, s2x, s2y, r2z, r2x, r2y, s3z, s3x, s3y, r3z, r3x, r3y,
    fin, fin_in,
    loc, ysem, xsem, zsem, csem, lsem, dsem, sem1, sem2, sem3, fsem,
):
    ops, blk = lax.axis_index("ops"), lax.axis_index("blk")
    z, xh, core = ops // 4, (ops // 2) % 2, ops % 2
    y, xl = blk // 2, blk % 2
    x, e = xh * 2 + xl, z % 2

    def device(dz=0, dx=0, dy=0, dc=0):
        zz, xx, yy, cc = (z + dz) % 4, (x + dx) % 4, (y + dy) % 4, (core + dc) % 2
        return (zz * 4 + (xx // 2) * 2 + cc, yy * 2 + xx % 2)

    def mate(dy, flip):
        return (ops, ((y + dy) % 4) * 2 + (xl + flip) % 2)

    sent = []

    def send(src, dst, send_sem, recv_sem, to):
        copy = pltpu.make_async_remote_copy(
            src_ref=src, dst_ref=dst, send_sem=send_sem, recv_sem=recv_sem, device_id=to, device_id_type=MESH
        )
        copy.start()
        sent.append(copy)

    def arrived(dst, sem):
        pltpu.make_async_remote_copy(
            src_ref=dst, dst_ref=dst, send_sem=sem, recv_sem=sem, device_id=device(dc=1), device_id_type=MESH
        ).wait_recv()

    in_psi = pltpu.make_async_copy(psi, states.at[pl.ds(blk * 8, 8)], loc.at[0])
    in_left = pltpu.make_async_copy(left, lin, loc.at[1])
    in_right = pltpu.make_async_copy(right, rops, loc.at[2])
    in_psi.start()
    in_left.start()
    in_right.start()

    barrier = pltpu.get_barrier_semaphore()
    peers = [device(dc=1)]
    for d in (1, 2, 3):
        peers += [device(dz=d), device(dx=d), device(dy=d), mate(d, 1)]
    for peer in peers:
        pl.semaphore_signal(barrier, inc=1, device_id=peer, device_id_type=MESH)

    in_left.wait()
    lane = lax.broadcasted_iota(jnp.int32, (128, 128), 1)
    masks = [jnp.where(lane < lens[2 * blk + k], 1.0, 0.0).astype(BF16) for k in range(2)]

    @pl.loop(0, 8)
    def _(c):
        for i in range(2):
            for k in range(2):
                lsend[c, i * 2 + k] = lin[lax.rem(partner[c * 2 + i], 16), k] * masks[k]

    lrecv[blk] = lsend[blk]
    in_psi.wait()
    pl.semaphore_wait(barrier, len(peers))

    ys = [0, 3, 1, 2]

    def unit(j, flip, parity, half, k, n=1):
        c = ((y + ys[j]) % 4) * 2 + (xl + flip) % 2
        return states.at[pl.ds(((c * 2 + parity) * 2 + half) * 2 + k, n)]

    mine = lambda j, flip, k, n=1: unit(j, flip, e, core, k, n)

    send(mine(0, 0, 0, 2), mine(0, 0, 0, 2), ysem.at[0, 0], ysem.at[1, 0], device(dy=1))
    send(mine(0, 0, 0, 2), mine(0, 0, 0, 2), ysem.at[0, 1], ysem.at[1, 1], device(dy=3))

    def x_out(j, k):
        send(mine(j, 0, k), mine(j, 0, k), xsem.at[0, j, k], xsem.at[1, j, k], device(dx=1 if k == 0 else 3))

    def z_out(flip, j, k):
        n = flip * 4 + j
        send(mine(j, flip, k), mine(j, flip, k), zsem.at[0, n, k], zsem.at[1, n, k], device(dz=1 if k == 0 else 3))

    def c_out(flip, j, other):
        n = flip * 4 + j
        ref = unit(j, flip, (e + other) % 2, core, 0, 2)
        send(ref, ref, csem.at[0, n, other], csem.at[1, n, other], device(dc=1))

    def l_out(dy, flip):
        n = dy * 2 + flip
        to = ((y + dy) % 4) * 2 + (xl + flip) % 2
        send(lsend.at[to], lrecv.at[blk], lsem.at[0, n], lsem.at[1, n], mate(dy, flip))

    x_out(0, 0)
    x_out(0, 1)
    l_out(0, 1)
    arrived(mine(1, 0, 0, 2), ysem.at[1, 0])
    send(mine(1, 0, 0), mine(1, 0, 0), ysem.at[0, 2], ysem.at[1, 2], device(dy=1))
    for k in range(2):
        x_out(1, k)
        z_out(0, 1, k)
    c_out(0, 1, 0)
    arrived(mine(2, 0, 0, 2), ysem.at[1, 1])
    send(mine(2, 0, 1), mine(2, 0, 1), ysem.at[0, 3], ysem.at[1, 3], device(dy=3))
    for k in range(2):
        x_out(2, k)
        z_out(0, 2, k)
    c_out(0, 2, 0)
    for dy, flip in ((1, 0), (3, 0), (2, 0), (1, 1), (3, 1), (2, 1)):
        l_out(dy, flip)
    for k in range(2):
        arrived(mine(0, 1, k), xsem.at[1, 0, k])
        z_out(1, 0, k)
    c_out(1, 0, 0)
    for k in range(2):
        arrived(mine(3, 0, k), ysem.at[1, 2 + k])
        x_out(3, k)
        z_out(0, 3, k)
    c_out(0, 3, 0)
    for j in (1, 2, 3):
        for k in range(2):
            arrived(mine(j, 1, k), xsem.at[1, j, k])
            z_out(1, j, k)
        c_out(1, j, 0)
    pieces = [(0, 1), (0, 2), (1, 0), (0, 3), (1, 1), (1, 2), (1, 3)]
    for flip, j in pieces:
        for k in range(2):
            arrived(unit(j, flip, (e + 1) % 2, core, k), zsem.at[1, flip * 4 + j, k])
        c_out(flip, j, 1)
    for flip, j in pieces:
        for other in range(2):
            arrived(unit(j, flip, (e + other) % 2, (core + 1) % 2, 0, 2), csem.at[1, flip * 4 + j, other])
    in_right.wait()

    @pl.loop(0, 8)
    def _(c):
        rows = states[pl.ds(c * 8, 8)].reshape(256, 1024)
        for i in range(2):
            for n in range(4):
                made = jnp.dot(rows, rops[i, :, n * 256 : n * 256 + 256], preferred_element_type=F32).astype(BF16)
                for k in range(2):
                    image[n, c * 4 + i * 2 + k] = made[k * 128 : k * 128 + 128]

    for dy in range(4):
        for flip in range(2):
            if dy or flip:
                source = ((y - dy) % 4) * 2 + (xl + flip) % 2
                arrived(lrecv.at[source], lsem.at[1, dy * 2 + flip])

    def mix(zi):
        chunk = (z + 1 + zi) % 4

        def group(g, acc):
            for u in range(8):
                p = g * 8 + u
                at = table[p]
                keep = table[32 + p].astype(F32)
                acc = acc * keep + jnp.dot(
                    lrecv[at // 4, at % 4], image[chunk, at], preferred_element_type=F32
                )
                runs[zi % 2, p] = acc.astype(BF16)
            return acc

        lax.fori_loop(0, 4, group, jnp.zeros((128, 256), F32))

    def total(zi, t):
        value = runs[zi % 2, table[64 + t]].astype(F32)
        return value * table[96 + t].astype(F32)

    def swap(zi):
        @pl.loop(0, 8)
        def _(c):
            dsend[zi, c] = total(zi, 2 * c + 1 - core).astype(BF16)

    def swap_out(zi):
        send(dsend.at[zi], drecv.at[zi], dsem.at[0, zi], dsem.at[1, zi], device(dc=1))

    def join(zi):
        arrived(drecv.at[zi], dsem.at[1, zi])

        @pl.loop(0, 4)
        def _(yd):
            for xld in range(2):
                c = yd * 2 + xld
                value = (total(zi, 2 * c + core) + drecv[zi, c].astype(F32)).astype(BF16)
                for xhd in range(2):
                    part = value[:, xhd * 128 : xhd * 128 + 128]
                    s1z[zi, (xhd * 2 + xld) * 4 + yd] = part[:PZ]
                    s1x[xhd * 2 + xld, zi, yd] = part[PZ : PZ + PX]
                    s1y[yd, zi, xhd * 2 + xld] = part[PZ + PX :]

    def first_out(zi):
        for d in (1, 2, 3):
            send(s1x.at[(x + d) % 4, zi], r1x.at[d - 1, zi], sem1.at[0, 1, d - 1, zi], sem1.at[1, 1, d - 1, zi], device(dx=d))
            send(s1y.at[(y + d) % 4, zi], r1y.at[d - 1, zi], sem1.at[0, 2, d - 1, zi], sem1.at[1, 2, d - 1, zi], device(dy=d))
        if zi < 3:
            send(s1z.at[zi], r1z.at[zi], sem1.at[0, 0, zi, 0], sem1.at[1, 0, zi, 0], device(dz=zi + 1))

    for zi in range(4):
        mix(zi)
        swap(zi)
        if zi >= 1:
            join(zi - 1)
        swap_out(zi)
        if zi >= 1:
            first_out(zi - 1)
    join(3)
    first_out(3)

    def summed(own, others):
        value = own.astype(F32)
        for other in others:
            value = value + other.astype(F32)
        return value

    for d in range(3):
        arrived(r1z.at[d], sem1.at[1, 0, d, 0])

    @pl.loop(0, 16)
    def _(b):
        s2z[b // 4, b % 4] = summed(s1z[3, b], [r1z[d, b] for d in range(3)]).astype(BF16)

    for d in range(3):
        for zi in range(4):
            arrived(r1x.at[d, zi], sem1.at[1, 1, d, zi])

    @pl.loop(0, 4)
    def _(zi):
        for yd in range(4):
            s2x[yd, zi] = summed(s1x[x, zi, yd], [r1x[d, zi, yd] for d in range(3)]).astype(BF16)

    for d in (1, 2, 3):
        send(s2z.at[(x + d) % 4], r2z.at[d - 1], sem2.at[0, 0, d - 1], sem2.at[1, 0, d - 1], device(dx=d))
    for d in range(3):
        for zi in range(4):
            arrived(r1y.at[d, zi], sem1.at[1, 2, d, zi])

    @pl.loop(0, 4)
    def _(zi):
        for b in range(4):
            s2y[zi, b] = summed(s1y[y, zi, b], [r1y[d, zi, b] for d in range(3)]).astype(BF16)

    for d in (1, 2, 3):
        send(s2x.at[(y + d) % 4], r2x.at[d - 1], sem2.at[0, 1, d - 1], sem2.at[1, 1, d - 1], device(dy=d))

    for d in range(3):
        arrived(r2z.at[d], sem2.at[1, 0, d])
    for yd in range(4):
        s3z[yd] = summed(s2z[x, yd], [r2z[d, yd] for d in range(3)]).astype(BF16)
    for d in range(3):
        send(s2y.at[d], r2y.at[d], sem2.at[0, 2, d], sem2.at[1, 2, d], device(dz=d + 1))
    for d in range(3):
        arrived(r2x.at[d], sem2.at[1, 1, d])
    for zi in range(4):
        s3x[zi] = summed(s2x[y, zi], [r2x[d, zi] for d in range(3)]).astype(BF16)
    for d in (1, 2, 3):
        send(s3z.at[(y + d) % 4], r3z.at[d - 1], sem3.at[0, 0, d - 1], sem3.at[1, 0, d - 1], device(dy=d))
    for d in range(3):
        arrived(r2y.at[d], sem2.at[1, 2, d])
    for b in range(4):
        s3y[b] = summed(s2y[3, b], [r2y[d, b] for d in range(3)]).astype(BF16)
    for d in range(3):
        send(s3x.at[d], r3x.at[d], sem3.at[0, 1, d], sem3.at[1, 1, d], device(dz=d + 1))

    row = lax.broadcasted_iota(jnp.int32, (128, 128), 0)
    live = row < lens[2 * blk + core]
    for d in range(3):
        arrived(r3z.at[d], sem3.at[1, 0, d])
    top = summed(s3z[y], [r3z[d] for d in range(3)])
    for d in (1, 2, 3):
        send(s3y.at[(x + d) % 4], r3y.at[d - 1], sem3.at[0, 2, d - 1], sem3.at[1, 2, d - 1], device(dx=d))
    for d in range(3):
        arrived(r3x.at[d], sem3.at[1, 1, d])
    middle = summed(s3x[3], [r3x[d] for d in range(3)])
    for d in range(3):
        arrived(r3y.at[d], sem3.at[1, 2, d])
    bottom = summed(s3y[x], [r3y[d] for d in range(3)])
    value = jnp.where(live, jnp.concatenate([top, middle, bottom], axis=0), 0.0)
    fin[...] = value.astype(BF16)
    send(fin, fin_in, fsem.at[0], fsem.at[1], device(dc=1))
    pick = lambda a: jnp.where(core == 0, a[:, :64], a[:, 64:])
    out[pl.ds(core * 128, 128), :] = pick(value).astype(BF16)
    arrived(fin_in, fsem.at[1])
    out[pl.ds((1 - core) * 128, 128), :] = pick(fin_in[...].astype(F32)).astype(BF16)
    for copy in sent:
        copy.wait_send()


def local(psi, left_blocks, right_ops, block_target, left_partner, block_len):
    smem = pl.BlockSpec(memory_space=SMEM)
    hbm = pl.BlockSpec(memory_space=pl.ANY)
    table = pl.pallas_call(
        order_kernel,
        name="order",
        out_shape=jax.ShapeDtypeStruct((128,), jnp.int32),
        in_specs=[smem, smem],
        out_specs=smem,
        scratch_shapes=[SMEM((16,), jnp.int32)],
    )(left_partner, block_target)
    b = lambda *shape: VMEM(shape, BF16)
    return pl.pallas_call(
        kernel,
        name="sigma",
        out_shape=jax.ShapeDtypeStruct((256, 64), BF16),
        in_specs=[smem, smem, smem, hbm, hbm, hbm],
        out_specs=pl.BlockSpec(memory_space=VMEM),
        scratch_shapes=[
            b(64, 32, 1024), b(8, 4, 128, 128), b(8, 4, 128, 128), b(16, 2, 128, 128), b(2, 1024, 1024),
            b(4, 32, 128, 256), b(2, 32, 128, 256), b(4, 8, 128, 256), b(4, 8, 128, 256),
            b(4, 16, PZ, 128), b(4, 4, 4, PX, 128), b(4, 4, 4, PY, 128),
            b(3, 16, PZ, 128), b(3, 4, 4, PX, 128), b(3, 4, 4, PY, 128),
            b(4, 4, PZ, 128), b(4, 4, PX, 128), b(4, 4, PY, 128),
            b(3, 4, PZ, 128), b(3, 4, PX, 128), b(3, 4, PY, 128),
            b(4, PZ, 128), b(4, PX, 128), b(4, PY, 128),
            b(3, PZ, 128), b(3, PX, 128), b(3, PY, 128),
            b(128, 128), b(128, 128),
            DMA((3,)), DMA((2, 4)), DMA((2, 4, 2)), DMA((2, 8, 2)), DMA((2, 8, 2)), DMA((2, 8)), DMA((2, 4)),
            DMA((2, 3, 3, 4)), DMA((2, 3, 3)), DMA((2, 3, 3)), DMA((2,)),
        ],
        compiler_params=pltpu.CompilerParams(
            collective_id=0, has_side_effects=True, vmem_limit_bytes=60 << 20
        ),
    )(left_partner, block_len, table, psi.reshape(8, 32, 1024), left_blocks, right_ops)


def solution(mesh):
    return jax.shard_map(
        local,
        mesh=mesh,
        in_specs=(
            P("blk", None),
            P("ops", "blk", None, None),
            P(("ops", "blk"), None, None),
            P("ops", None),
            P("ops"),
            P(),
        ),
        out_specs=P("blk", "ops"),
        check_vma=False,
    )
```

time: 561 us -> 78.1 us (0.14); the launches traced: 555 us -> 77.9 us
  waiting for transfers between devices: 344 us -> 0 us
  Pallas kernels: 0 us -> 76.4 us
  other arithmetic: 70.4 us -> 0 us
  loops' own time: 61.6 us -> 0 us
  local copies, waits for them, and re-layouts: 29.7 us -> 1.54 us
  matrix products: 25.9 us -> 0 us
  between operations: 13.1 us -> 0.02 us
  blocking collectives: 9.94 us -> 0 us
    all_gather x2 -> x0, waiting for transfers between devices: 263 us -> none  [the longest x1 170 us: local(): lax.all_gather(left_blocks, 'blk', axis=1, tiled=True)]
    unnamed x4 -> x0, waiting for transfers between devices: 81.4 us -> none
    pallas_call x0 -> x2, Pallas kernels: none -> 76.4 us  [the longest x1 74.5 us: local(): pl.pallas_call(kernel, name='sigma', out_shape=jax.ShapeDtypeStruct((256,...]
    dynamic_update_slice x32 -> x0, other arithmetic: 61.7 us -> none  [add_blocks(): lax.dynamic_update_index_in_dim(running, current + mixed[source], where, 0)]
    another operation x1 -> x0, loops' own time: 61.6 us -> none  [local(): partial_sum = lax.fori_loop(0, local_ops, apply_own, blank)]
    dot_general x4 -> x0, matrix products: 25.9 us -> none  [the longest x2 18.7 us: apply_own(): jnp.dot(stacked, right_ops[step], preferred_element_type=jnp.float32)]
    reshape x3 -> x0, local copies, waits for them, and re-layouts: 13 us -> none  [the longest x2 12.8 us: apply_own(): image = image.reshape(blocks_all, block_rows, columns)]
    all_to_all x1 -> x0, blocking collectives: 9.94 us -> none  [sent_and_summed(): lax.all_to_all(tiles, axis, split_axis=0, concat_axis=0, tiled=True)]
  transfers between devices with their start and end apart: 3 -> 0, of which waited for: 3 -> 0; matrix products, arithmetic and copies ran while one was open for 0% -> 0% of each run, Pallas kernels for 0% -> 0%
where the time goes in v1:
time: 78.1 us; the launch traced here: 77.9 us
  Pallas kernels  76.4 us (98%)
  local copies, waits for them, and re-layouts  1.54 us (2%)
    pallas_call x1, Pallas kernels, local(): pl.pallas_call(kernel, name='sigma', out_shape=jax.ShapeDtypeStruct((256,...  74.5 us
    pallas_call x1, Pallas kernels, local(): pl.pallas_call(order_kernel, name='order', out_shape=jax.ShapeDtypeStruct...  1.84 us

profile of v1, /device:TPU:1, one launch (start us, length us, event | category | flops | bytes accessed | tf_op | source)
XLA Modules:
  0.0 77.9 jit_solution(5654327492693920200)
XLA Ops:
  0.0 1.8 %order.1.table = s32[128]{0:T(128)} custom-call(s32[16]{0:T(128)} %partner.3, s32[16,16]{1,0:T(8,128)} %targets.1), custom_call_target="tpu_custom_call" | custom-call | tf_op jit(solution)/shard_map/order/pallas_call | solution.py:334
  1.9 74.5 %sigma.1 = bf16[256,64]{1,0:T(8,128)(2,1)} custom-call(s32[16]{0:T(128)} %partner.3, s32[16]{0:T(128)} %lens.1, s32[128]{0:T(128)} %order.1.table, bf16[8,32,1024]{2,1,0:T(8,128)(2,1)} %bitcast.1, bf16[16,2,128,128]{3,2,1,0:T(8,128)(2,1)} %left.1, bf16[2,1024,1024]{2,1,0:T(8,128)(2,1)} %right.1), custom_call_target="tpu_custom_call" | custom-call | tf_op jit(solution)/shard_map/sigma/pallas_call | solution.py:343
  76.4 1.5 %copy.7 = bf16[256,64]{0,1:T(8,128)(2,1)} copy(bf16[256,64]{1,0:T(8,128)(2,1)} %sigma.1) | data formatting | bytes 65536 | tf_op jit(solution)/shard_map/sigma/pallas_call | solution.py:343

commit v2 on v1

--- a/solution.py
+++ b/solution.py
@@ -11,44 +11,12 @@
 PZ, PX, PY = 48, 48, 32
 
 
-def order_kernel(partner, targets, table, fill):
-    blk = lax.axis_index("blk")
-    owners = [lax.rem(partner[blk * 2 + i], 16) for i in range(2)]
-    for t in range(16):
-        fill[t] = 0
-
-    @pl.loop(0, 8)
-    def _(c):
-        for i in range(2):
-            for e in range(2):
-                t = targets[owners[i], 2 * c + e]
-                fill[t] = fill[t] + 1
-
-    begin = jnp.int32(0)
-    for t in range(16):
-        count = fill[t]
-        fill[t] = begin
-        table[80 + t] = begin
-        table[96 + t] = jnp.where(count > 0, 1, 0)
-        begin = begin + count
-        table[64 + t] = jnp.maximum(begin - 1, 0)
-
-    @pl.loop(0, 8)
-    def _(c):
-        for i in range(2):
-            for e in range(2):
-                t = targets[owners[i], 2 * c + e]
-                at = fill[t]
-                table[at] = c * 4 + i * 2 + e
-                table[32 + at] = jnp.where(at > table[80 + t], 1, 0)
-                fill[t] = at + 1
-
-
 def kernel(
-    partner, lens, table, psi, left, right, out,
+    partner, lens, targets, psi, left, right, out,
     states, lsend, lrecv, lin, rops, image, runs, dsend, drecv,
     s1z, s1x, s1y, r1z, r1x, r1y, s2z, s2x, s2y, r2z, r2x, r2y, s3z, s3x, s3y, r3z, r3x, r3y,
     fin, fin_in,
+    order, table,
     loc, ysem, xsem, zsem, csem, lsem, dsem, sem1, sem2, sem3, fsem,
 ):
     ops, blk = lax.axis_index("ops"), lax.axis_index("blk")
@@ -77,6 +45,12 @@
             src_ref=dst, dst_ref=dst, send_sem=sem, recv_sem=sem, device_id=device(dc=1), device_id_type=MESH
         ).wait_recv()
 
+    barrier = pltpu.get_barrier_semaphore()
+    peers = [device(dc=1)]
+    for d in (1, 2, 3):
+        peers += [device(dz=d), device(dx=d), device(dy=d), mate(d, 1)]
+    for peer in peers:
+        pl.semaphore_signal(barrier, inc=1, device_id=peer, device_id_type=MESH)
     in_psi = pltpu.make_async_copy(psi, states.at[pl.ds(blk * 8, 8)], loc.at[0])
     in_left = pltpu.make_async_copy(left, lin, loc.at[1])
     in_right = pltpu.make_async_copy(right, rops, loc.at[2])
@@ -84,12 +58,86 @@
     in_left.start()
     in_right.start()
 
-    barrier = pltpu.get_barrier_semaphore()
-    peers = [device(dc=1)]
-    for d in (1, 2, 3):
-        peers += [device(dz=d), device(dx=d), device(dy=d), mate(d, 1)]
-    for peer in peers:
-        pl.semaphore_signal(barrier, inc=1, device_id=peer, device_id_type=MESH)
+    ys = [0, 3, 1, 2]
+
+    def unit(j, flip, parity, half, k, n=1):
+        c = ((y + ys[j]) % 4) * 2 + (xl + flip) % 2
+        return states.at[pl.ds(((c * 2 + parity) * 2 + half) * 2 + k, n)]
+
+    mine = lambda j, flip, k, n=1: unit(j, flip, e, core, k, n)
+
+    def y_out(n, j, k, dy):
+        send(mine(j, 0, k), mine(j, 0, k), ysem.at[0, n], ysem.at[1, n], device(dy=dy))
+
+    def x_out(j, k):
+        send(mine(j, 0, k), mine(j, 0, k), xsem.at[0, j, k], xsem.at[1, j, k], device(dx=1 if k == 0 else 3))
+
+    def z_out(flip, j, k):
+        n = flip * 4 + j
+        send(mine(j, flip, k), mine(j, flip, k), zsem.at[0, n, k], zsem.at[1, n, k], device(dz=1 if k == 0 else 3))
+
+    def c_out(flip, j, other):
+        n = flip * 4 + j
+        ref = unit(j, flip, (e + other) % 2, core, 0, 2)
+        send(ref, ref, csem.at[0, n, other], csem.at[1, n, other], device(dc=1))
+
+    def l_out(dy, flip):
+        n = dy * 2 + flip
+        to = ((y + dy) % 4) * 2 + (xl + flip) % 2
+        send(lsend.at[to], lrecv.at[blk], lsem.at[0, n], lsem.at[1, n], mate(dy, flip))
+
+    def images(*blocks):
+        at = [(((y + ys[j]) % 4) * 2 + (xl + flip) % 2) * 2 + (e + other) % 2 for flip, j, other in blocks]
+
+        @pl.loop(0, 2)
+        def _(i):
+            rows = jnp.concatenate([states[pl.ds(q * 4, 4)].reshape(128, 1024) for q in at], axis=0)
+            for n in range(4):
+                made = jnp.dot(rows, rops[i, :, n * 256 : n * 256 + 256], preferred_element_type=F32).astype(BF16)
+                for k in range(2):
+                    image[n, i * 16 + at[k]] = made[k * 128 : k * 128 + 128]
+
+    def images_of(*blocks):
+        for flip, j, other in blocks:
+            arrived(unit(j, flip, (e + other) % 2, (core + 1) % 2, 0, 2), csem.at[1, flip * 4 + j, other])
+        images(*blocks)
+
+    number = lambda cond: jnp.where(cond, 1, 0)
+    kk = lax.broadcasted_iota(jnp.int32, (32, 128), 0)
+    lane = lax.broadcasted_iota(jnp.int32, (32, 128), 1)
+    owners = [lax.rem(partner[blk * 2 + i], 16) for i in range(2)]
+    goals = [targets[owners[i], q] for i in range(2) for q in range(16)]
+    goal = jnp.zeros((32, 128), jnp.int32)
+    for at in range(32):
+        goal = jnp.where(kk == at, goals[at], goal)
+    key = goal * 32 + kk
+    rank, again = jnp.zeros((32, 128), jnp.int32), jnp.zeros((32, 128), jnp.int32)
+    for at in range(32):
+        rank = rank + number(key > goals[at] * 32 + at)
+        again = again + number((goal == goals[at]) & (kk > at))
+    place = rank == lane
+    left_at = (kk % 16 // 2) * 4 + (kk // 16) * 2 + kk % 2
+
+    def down_sum(value):
+        value = value[:8] + value[8:16] + value[16:24] + value[24:]
+        return sum(value[r : r + 1] for r in range(1, 8)) + value[:1]
+
+    rows = [
+        down_sum(jnp.where(place, kk, 0)), down_sum(jnp.where(place, left_at, 0)),
+        down_sum(number(place & (again > 0))), jnp.maximum(down_sum(number(goal <= lane)) - 1, 0),
+        jnp.minimum(down_sum(number(goal == lane)), 1), jnp.zeros((3, 128), jnp.int32),
+    ]
+    order[...] = jnp.concatenate(rows, axis=0)
+    order_out = pltpu.make_async_copy(order, table, loc.at[3])
+
+    in_psi.wait()
+    pl.semaphore_wait(barrier, len(peers))
+    y_out(0, 0, 0, 1)
+    y_out(1, 0, 1, 3)
+    x_out(0, 0)
+    x_out(0, 1)
+    y_out(2, 0, 1, 1)
+    y_out(3, 0, 0, 3)
 
     in_left.wait()
     lane = lax.broadcasted_iota(jnp.int32, (128, 128), 1)
@@ -102,92 +150,70 @@
                 lsend[c, i * 2 + k] = lin[lax.rem(partner[c * 2 + i], 16), k] * masks[k]
 
     lrecv[blk] = lsend[blk]
-    in_psi.wait()
-    pl.semaphore_wait(barrier, len(peers))
-
-    ys = [0, 3, 1, 2]
-
-    def unit(j, flip, parity, half, k, n=1):
-        c = ((y + ys[j]) % 4) * 2 + (xl + flip) % 2
-        return states.at[pl.ds(((c * 2 + parity) * 2 + half) * 2 + k, n)]
-
-    mine = lambda j, flip, k, n=1: unit(j, flip, e, core, k, n)
-
-    send(mine(0, 0, 0, 2), mine(0, 0, 0, 2), ysem.at[0, 0], ysem.at[1, 0], device(dy=1))
-    send(mine(0, 0, 0, 2), mine(0, 0, 0, 2), ysem.at[0, 1], ysem.at[1, 1], device(dy=3))
-
-    def x_out(j, k):
-        send(mine(j, 0, k), mine(j, 0, k), xsem.at[0, j, k], xsem.at[1, j, k], device(dx=1 if k == 0 else 3))
-
-    def z_out(flip, j, k):
-        n = flip * 4 + j
-        send(mine(j, flip, k), mine(j, flip, k), zsem.at[0, n, k], zsem.at[1, n, k], device(dz=1 if k == 0 else 3))
-
-    def c_out(flip, j, other):
-        n = flip * 4 + j
-        ref = unit(j, flip, (e + other) % 2, core, 0, 2)
-        send(ref, ref, csem.at[0, n, other], csem.at[1, n, other], device(dc=1))
-
-    def l_out(dy, flip):
-        n = dy * 2 + flip
-        to = ((y + dy) % 4) * 2 + (xl + flip) % 2
-        send(lsend.at[to], lrecv.at[blk], lsem.at[0, n], lsem.at[1, n], mate(dy, flip))
-
-    x_out(0, 0)
-    x_out(0, 1)
     l_out(0, 1)
-    arrived(mine(1, 0, 0, 2), ysem.at[1, 0])
-    send(mine(1, 0, 0), mine(1, 0, 0), ysem.at[0, 2], ysem.at[1, 2], device(dy=1))
-    for k in range(2):
-        x_out(1, k)
-        z_out(0, 1, k)
+    order_out.start()
+    in_right.wait()
+
+    def from_y(j, k, n):
+        arrived(mine(j, 0, k), ysem.at[1, n])
+        x_out(j, k)
+        z_out(0, j, k)
+
+    def from_x(j, k):
+        arrived(mine(j, 1, k), xsem.at[1, j, k])
+        z_out(1, j, k)
+
+    def from_z(flip, j):
+        for k in range(2):
+            arrived(unit(j, flip, (e + 1) % 2, core, k), zsem.at[1, flip * 4 + j, k])
+        c_out(flip, j, 1)
+
+    images((0, 0, 0), (0, 0, 1))
+    from_y(1, 0, 0)
+    y_out(4, 1, 0, 1)
+    from_y(2, 1, 1)
+    y_out(5, 2, 1, 3)
+    from_x(0, 0)
+    from_x(0, 1)
+    c_out(1, 0, 0)
+    from_y(1, 1, 2)
     c_out(0, 1, 0)
-    arrived(mine(2, 0, 0, 2), ysem.at[1, 1])
-    send(mine(2, 0, 1), mine(2, 0, 1), ysem.at[0, 3], ysem.at[1, 3], device(dy=3))
-    for k in range(2):
-        x_out(2, k)
-        z_out(0, 2, k)
+    from_y(2, 0, 3)
     c_out(0, 2, 0)
     for dy, flip in ((1, 0), (3, 0), (2, 0), (1, 1), (3, 1), (2, 1)):
         l_out(dy, flip)
-    for k in range(2):
-        arrived(mine(0, 1, k), xsem.at[1, 0, k])
-        z_out(1, 0, k)
-    c_out(1, 0, 0)
-    for k in range(2):
-        arrived(mine(3, 0, k), ysem.at[1, 2 + k])
-        x_out(3, k)
-        z_out(0, 3, k)
+    images_of((1, 0, 0), (0, 1, 0))
+    from_y(3, 0, 4)
+    from_y(3, 1, 5)
     c_out(0, 3, 0)
-    for j in (1, 2, 3):
-        for k in range(2):
-            arrived(mine(j, 1, k), xsem.at[1, j, k])
-            z_out(1, j, k)
-        c_out(1, j, 0)
-    pieces = [(0, 1), (0, 2), (1, 0), (0, 3), (1, 1), (1, 2), (1, 3)]
-    for flip, j in pieces:
-        for k in range(2):
-            arrived(unit(j, flip, (e + 1) % 2, core, k), zsem.at[1, flip * 4 + j, k])
-        c_out(flip, j, 1)
-    for flip, j in pieces:
-        for other in range(2):
-            arrived(unit(j, flip, (e + other) % 2, (core + 1) % 2, 0, 2), csem.at[1, flip * 4 + j, other])
-    in_right.wait()
-
-    @pl.loop(0, 8)
-    def _(c):
-        rows = states[pl.ds(c * 8, 8)].reshape(256, 1024)
-        for i in range(2):
-            for n in range(4):
-                made = jnp.dot(rows, rops[i, :, n * 256 : n * 256 + 256], preferred_element_type=F32).astype(BF16)
-                for k in range(2):
-                    image[n, c * 4 + i * 2 + k] = made[k * 128 : k * 128 + 128]
-
+    from_x(1, 0)
+    from_x(2, 1)
+    from_x(1, 1)
+    c_out(1, 1, 0)
+    from_x(2, 0)
+    c_out(1, 2, 0)
+    from_z(0, 1)
+    from_z(0, 2)
+    images_of((0, 2, 0), (0, 3, 0))
+    from_x(3, 0)
+    from_x(3, 1)
+    c_out(1, 3, 0)
+    from_z(1, 0)
+    images_of((0, 1, 1), (0, 2, 1))
+    from_z(0, 3)
+    images_of((1, 1, 0), (1, 2, 0))
+    from_z(1, 1)
+    from_z(1, 2)
+    images_of((1, 0, 1), (0, 3, 1))
+    from_z(1, 3)
+    images_of((1, 1, 1), (1, 2, 1))
+    images_of((1, 3, 0), (1, 3, 1))
+    order_out.wait()
     for dy in range(4):
         for flip in range(2):
             if dy or flip:
-                source = ((y - dy) % 4) * 2 + (xl + flip) % 2
-                arrived(lrecv.at[source], lsem.at[1, dy * 2 + flip])
+                source_at = ((y - dy) % 4) * 2 + (xl + flip) % 2
+                arrived(lrecv.at[source_at], lsem.at[1, dy * 2 + flip])
 
     def mix(zi):
         chunk = (z + 1 + zi) % 4
@@ -195,10 +221,9 @@
         def group(g, acc):
             for u in range(8):
                 p = g * 8 + u
-                at = table[p]
-                keep = table[32 + p].astype(F32)
+                keep = table[2, p].astype(F32)
                 acc = acc * keep + jnp.dot(
-                    lrecv[at // 4, at % 4], image[chunk, at], preferred_element_type=F32
+                    lrecv[table[1, p] // 4, table[1, p] % 4], image[chunk, table[0, p]], preferred_element_type=F32
                 )
                 runs[zi % 2, p] = acc.astype(BF16)
             return acc
@@ -206,8 +231,8 @@
         lax.fori_loop(0, 4, group, jnp.zeros((128, 256), F32))
 
     def total(zi, t):
-        value = runs[zi % 2, table[64 + t]].astype(F32)
-        return value * table[96 + t].astype(F32)
+        value = runs[zi % 2, table[3, t]].astype(F32)
+        return value * table[4, t].astype(F32)
 
     def swap(zi):
         @pl.loop(0, 8)
@@ -331,14 +356,6 @@
 def local(psi, left_blocks, right_ops, block_target, left_partner, block_len):
     smem = pl.BlockSpec(memory_space=SMEM)
     hbm = pl.BlockSpec(memory_space=pl.ANY)
-    table = pl.pallas_call(
-        order_kernel,
-        name="order",
-        out_shape=jax.ShapeDtypeStruct((128,), jnp.int32),
-        in_specs=[smem, smem],
-        out_specs=smem,
-        scratch_shapes=[SMEM((16,), jnp.int32)],
-    )(left_partner, block_target)
     b = lambda *shape: VMEM(shape, BF16)
     return pl.pallas_call(
         kernel,
@@ -356,13 +373,14 @@
             b(4, PZ, 128), b(4, PX, 128), b(4, PY, 128),
             b(3, PZ, 128), b(3, PX, 128), b(3, PY, 128),
             b(128, 128), b(128, 128),
-            DMA((3,)), DMA((2, 4)), DMA((2, 4, 2)), DMA((2, 8, 2)), DMA((2, 8, 2)), DMA((2, 8)), DMA((2, 4)),
+            VMEM((8, 128), jnp.int32), SMEM((8, 128), jnp.int32),
+            DMA((4,)), DMA((2, 6)), DMA((2, 4, 2)), DMA((2, 8, 2)), DMA((2, 8, 2)), DMA((2, 8)), DMA((2, 4)),
             DMA((2, 3, 3, 4)), DMA((2, 3, 3)), DMA((2, 3, 3)), DMA((2,)),
         ],
         compiler_params=pltpu.CompilerParams(
             collective_id=0, has_side_effects=True, vmem_limit_bytes=60 << 20
         ),
-    )(left_partner, block_len, table, psi.reshape(8, 32, 1024), left_blocks, right_ops)
+    )(left_partner, block_len, block_target, psi.reshape(8, 32, 1024), left_blocks, right_ops)
 
 
 def solution(mesh):

time: 78.1 us -> 69 us (0.88)
  Pallas kernels: 76.4 us -> 67.3 us
    pallas_call x1, Pallas kernels: 74.5 us -> 67.3 us  [local(): pl.pallas_call(kernel, name='sigma', out_shape=jax.ShapeDtypeStruct((256,...]
    pallas_call x1 -> x0, Pallas kernels: 1.84 us -> none  [local(): pl.pallas_call(order_kernel, name='order', out_shape=jax.ShapeDtypeStruct...]
where the time goes in v2:
time: 69 us; the launch traced here: 68.8 us
  Pallas kernels  67.3 us (98%)
  local copies, waits for them, and re-layouts  1.54 us (2%)
    pallas_call x1, Pallas kernels, local(): pl.pallas_call(kernel, name='sigma', out_shape=jax.ShapeDtypeStruct((256,...  67.3 us
    pallas_call x1, local copies, waits for them, and re-layouts, local(): pl.pallas_call(kernel, name='sigma', out_shape=jax.ShapeDtypeStruct((256,...  1.54 us

profile of v2, /device:TPU:1, one launch (start us, length us, event | category | flops | bytes accessed | tf_op | source)
XLA Modules:
  0.0 68.8 jit_solution(11999664335278713719)
XLA Ops:
  0.0 67.3 %sigma.1 = bf16[256,64]{1,0:T(8,128)(2,1)} custom-call(s32[16]{0:T(128)} %partner.1, s32[16]{0:T(128)} %lens.1, s32[16,16]{1,0:T(8,128)} %targets.1, bf16[8,32,1024]{2,1,0:T(8,128)(2,1)} %bitcast.1, bf16[16,2,128,128]{3,2,1,0:T(8,128)(2,1)} %left.1, bf16[2,1024,1024]{2,1,0:T(8,128)(2,1)} %right.1), custom_call_target="tpu_custom_call" | custom-call | tf_op jit(solution)/shard_map/sigma/pallas_call | solution.py:360
  67.3 1.5 %copy.7 = bf16[256,64]{0,1:T(8,128)(2,1)} copy(bf16[256,64]{1,0:T(8,128)(2,1)} %sigma.1) | data formatting | bytes 65536 | tf_op jit(solution)/shard_map/sigma/pallas_call | solution.py:360

commit v3 on v2

--- a/solution.py
+++ b/solution.py
@@ -8,16 +8,18 @@
 MESH = pl.DeviceIdType.MESH
 F32, BF16 = jnp.float32, jnp.bfloat16
 VMEM, SMEM, DMA = pltpu.VMEM, pltpu.SMEM, pltpu.SemaphoreType.DMA
-PZ, PX, PY = 48, 48, 32
+PZ, PX, PY = 32, 48, 48
+GROUP = 32
+ZR = (1, 3, 2, 0)
 
 
 def kernel(
     partner, lens, targets, psi, left, right, out,
     states, lsend, lrecv, lin, rops, image, runs, dsend, drecv,
     s1z, s1x, s1y, r1z, r1x, r1y, s2z, s2x, s2y, r2z, r2x, r2y, s3z, s3x, s3y, r3z, r3x, r3y,
-    fin, fin_in,
+    c3z, c3x, c3y,
     order, table,
-    loc, ysem, xsem, zsem, csem, lsem, dsem, sem1, sem2, sem3, fsem,
+    loc, ysem, xsem, zsem, csem, lsem, dsem, sem1, sem2, sem2x, sem3s, sem3r, fsem,
 ):
     ops, blk = lax.axis_index("ops"), lax.axis_index("blk")
     z, xh, core = ops // 4, (ops // 2) % 2, ops % 2
@@ -48,7 +50,7 @@
     barrier = pltpu.get_barrier_semaphore()
     peers = [device(dc=1)]
     for d in (1, 2, 3):
-        peers += [device(dz=d), device(dx=d), device(dy=d), mate(d, 1)]
+        peers += [device(dc=c, **{axis: d}) for axis in ("dz", "dx", "dy") for c in range(2)] + [mate(d, 1)]
     for peer in peers:
         pl.semaphore_signal(barrier, inc=1, device_id=peer, device_id_type=MESH)
     in_psi = pltpu.make_async_copy(psi, states.at[pl.ds(blk * 8, 8)], loc.at[0])
@@ -180,12 +182,15 @@
     c_out(0, 1, 0)
     from_y(2, 0, 3)
     c_out(0, 2, 0)
-    for dy, flip in ((1, 0), (3, 0), (2, 0), (1, 1), (3, 1), (2, 1)):
-        l_out(dy, flip)
+    l_out(1, 0)
+    l_out(3, 0)
+    l_out(2, 0)
     images_of((1, 0, 0), (0, 1, 0))
     from_y(3, 0, 4)
     from_y(3, 1, 5)
     c_out(0, 3, 0)
+    for dy in (1, 3, 2):
+        l_out(dy, 1)
     from_x(1, 0)
     from_x(2, 1)
     from_x(1, 1)
@@ -216,11 +221,11 @@
                 arrived(lrecv.at[source_at], lsem.at[1, dy * 2 + flip])
 
     def mix(zi):
-        chunk = (z + 1 + zi) % 4
+        chunk = (z + ZR[zi]) % 4
 
         def group(g, acc):
-            for u in range(8):
-                p = g * 8 + u
+            for u in range(GROUP):
+                p = g * GROUP + u
                 keep = table[2, p].astype(F32)
                 acc = acc * keep + jnp.dot(
                     lrecv[table[1, p] // 4, table[1, p] % 4], image[chunk, table[0, p]], preferred_element_type=F32
@@ -228,7 +233,7 @@
                 runs[zi % 2, p] = acc.astype(BF16)
             return acc
 
-        lax.fori_loop(0, 4, group, jnp.zeros((128, 256), F32))
+        lax.fori_loop(0, 32 // GROUP, group, jnp.zeros((128, 256), F32))
 
     def total(zi, t):
         value = runs[zi % 2, table[3, t]].astype(F32)
@@ -261,15 +266,14 @@
             send(s1x.at[(x + d) % 4, zi], r1x.at[d - 1, zi], sem1.at[0, 1, d - 1, zi], sem1.at[1, 1, d - 1, zi], device(dx=d))
             send(s1y.at[(y + d) % 4, zi], r1y.at[d - 1, zi], sem1.at[0, 2, d - 1, zi], sem1.at[1, 2, d - 1, zi], device(dy=d))
         if zi < 3:
-            send(s1z.at[zi], r1z.at[zi], sem1.at[0, 0, zi, 0], sem1.at[1, 0, zi, 0], device(dz=zi + 1))
+            send(s1z.at[zi], r1z.at[zi], sem1.at[0, 0, zi, 0], sem1.at[1, 0, zi, 0], device(dz=ZR[zi]))
 
     for zi in range(4):
         mix(zi)
         swap(zi)
+        swap_out(zi)
         if zi >= 1:
             join(zi - 1)
-        swap_out(zi)
-        if zi >= 1:
             first_out(zi - 1)
     join(3)
     first_out(3)
@@ -280,75 +284,88 @@
             value = value + other.astype(F32)
         return value
 
-    for d in range(3):
-        arrived(r1z.at[d], sem1.at[1, 0, d, 0])
-
-    @pl.loop(0, 16)
-    def _(b):
-        s2z[b // 4, b % 4] = summed(s1z[3, b], [r1z[d, b] for d in range(3)]).astype(BF16)
-
-    for d in range(3):
-        for zi in range(4):
+    def second_x(zi):
+        for d in range(3):
             arrived(r1x.at[d, zi], sem1.at[1, 1, d, zi])
-
-    @pl.loop(0, 4)
-    def _(zi):
         for yd in range(4):
             s2x[yd, zi] = summed(s1x[x, zi, yd], [r1x[d, zi, yd] for d in range(3)]).astype(BF16)
-
-    for d in (1, 2, 3):
-        send(s2z.at[(x + d) % 4], r2z.at[d - 1], sem2.at[0, 0, d - 1], sem2.at[1, 0, d - 1], device(dx=d))
-    for d in range(3):
-        for zi in range(4):
+        for d in (1, 2, 3):
+            send(s2x.at[(y + d) % 4, zi], r2x.at[d - 1, zi], sem2x.at[0, d - 1, zi], sem2x.at[1, d - 1, zi], device(dy=d))
+
+    def second_y(zi):
+        for d in range(3):
             arrived(r1y.at[d, zi], sem1.at[1, 2, d, zi])
-
-    @pl.loop(0, 4)
-    def _(zi):
         for b in range(4):
             s2y[zi, b] = summed(s1y[y, zi, b], [r1y[d, zi, b] for d in range(3)]).astype(BF16)
-
-    for d in (1, 2, 3):
-        send(s2x.at[(y + d) % 4], r2x.at[d - 1], sem2.at[0, 1, d - 1], sem2.at[1, 1, d - 1], device(dy=d))
-
+        if zi < 3:
+            send(s2y.at[zi], r2y.at[zi], sem2.at[0, 1, zi], sem2.at[1, 1, zi], device(dz=ZR[zi]))
+
+    def second_z():
+        for d in range(3):
+            arrived(r1z.at[d], sem1.at[1, 0, d, 0])
+        for xd in range(4):
+            for yd in range(4):
+                b = xd * 4 + yd
+                s2z[xd, yd] = summed(s1z[3, b], [r1z[d, b] for d in range(3)]).astype(BF16)
+        for d in (1, 2, 3):
+            send(s2z.at[(x + d) % 4], r2z.at[d - 1], sem2.at[0, 0, d - 1], sem2.at[1, 0, d - 1], device(dx=d))
+
+    def third_out(part, src, dst, d, axis):
+        for dc in range(2):
+            send(src, dst.at[core, d - 1], sem3s.at[part, dc, d - 1], sem3r.at[part, core, d - 1], device(**{axis: ZR[d - 1] if axis == "dz" else d, "dc": dc}))
+
+    def third_own(part, src, dst):
+        send(src, dst, fsem.at[0, part], fsem.at[1, part], device(dc=1))
+
+    def third_x(zi):
+        for d in range(3):
+            arrived(r2x.at[d, zi], sem2x.at[1, d, zi])
+        s3x[zi] = summed(s2x[y, zi], [r2x[d, zi] for d in range(3)]).astype(BF16)
+        if zi < 3:
+            third_out(1, s3x.at[zi], r3x, zi + 1, "dz")
+        else:
+            third_own(1, s3x.at[3], c3x)
+
+    second_x(0)
+    second_y(0)
+    second_x(1)
+    second_y(1)
+    second_z()
+    second_x(2)
+    second_y(2)
+    third_x(0)
+    second_x(3)
+    second_y(3)
+    third_x(1)
     for d in range(3):
         arrived(r2z.at[d], sem2.at[1, 0, d])
     for yd in range(4):
         s3z[yd] = summed(s2z[x, yd], [r2z[d, yd] for d in range(3)]).astype(BF16)
+    for d in (1, 2, 3):
+        third_out(0, s3z.at[(y + d) % 4], r3z, d, "dy")
+    third_own(0, s3z.at[y], c3z)
+    third_x(2)
     for d in range(3):
-        send(s2y.at[d], r2y.at[d], sem2.at[0, 2, d], sem2.at[1, 2, d], device(dz=d + 1))
-    for d in range(3):
-        arrived(r2x.at[d], sem2.at[1, 1, d])
-    for zi in range(4):
-        s3x[zi] = summed(s2x[y, zi], [r2x[d, zi] for d in range(3)]).astype(BF16)
-    for d in (1, 2, 3):
-        send(s3z.at[(y + d) % 4], r3z.at[d - 1], sem3.at[0, 0, d - 1], sem3.at[1, 0, d - 1], device(dy=d))
-    for d in range(3):
-        arrived(r2y.at[d], sem2.at[1, 2, d])
+        arrived(r2y.at[d], sem2.at[1, 1, d])
     for b in range(4):
         s3y[b] = summed(s2y[3, b], [r2y[d, b] for d in range(3)]).astype(BF16)
-    for d in range(3):
-        send(s3x.at[d], r3x.at[d], sem3.at[0, 1, d], sem3.at[1, 1, d], device(dz=d + 1))
+    for d in (1, 2, 3):
+        third_out(2, s3y.at[(x + d) % 4], r3y, d, "dx")
+    third_own(2, s3y.at[x], c3y)
+    third_x(3)
 
     row = lax.broadcasted_iota(jnp.int32, (128, 128), 0)
-    live = row < lens[2 * blk + core]
-    for d in range(3):
-        arrived(r3z.at[d], sem3.at[1, 0, d])
-    top = summed(s3z[y], [r3z[d] for d in range(3)])
-    for d in (1, 2, 3):
-        send(s3y.at[(x + d) % 4], r3y.at[d - 1], sem3.at[0, 2, d - 1], sem3.at[1, 2, d - 1], device(dx=d))
-    for d in range(3):
-        arrived(r3x.at[d], sem3.at[1, 1, d])
-    middle = summed(s3x[3], [r3x[d] for d in range(3)])
-    for d in range(3):
-        arrived(r3y.at[d], sem3.at[1, 2, d])
-    bottom = summed(s3y[x], [r3y[d] for d in range(3)])
-    value = jnp.where(live, jnp.concatenate([top, middle, bottom], axis=0), 0.0)
-    fin[...] = value.astype(BF16)
-    send(fin, fin_in, fsem.at[0], fsem.at[1], device(dc=1))
-    pick = lambda a: jnp.where(core == 0, a[:, :64], a[:, 64:])
-    out[pl.ds(core * 128, 128), :] = pick(value).astype(BF16)
-    arrived(fin_in, fsem.at[1])
-    out[pl.ds((1 - core) * 128, 128), :] = pick(fin_in[...].astype(F32)).astype(BF16)
+    for part, (got, own) in enumerate(((r3z, c3z), (r3x, c3x), (r3y, c3y))):
+        for d in range(3):
+            for half in range(2):
+                arrived(got.at[half, d], sem3r.at[part, half, d])
+        arrived(own, fsem.at[1, part])
+    for other in range(2):
+        half = (core + other) % 2
+        own = (c3z[...], c3x[...], c3y[...]) if other else (s3z[y], s3x[3], s3y[x])
+        parts = [summed(a, [got[half, d] for d in range(3)]) for a, got in zip(own, (r3z, r3x, r3y))]
+        value = jnp.where(row < lens[2 * blk + half], jnp.concatenate(parts, axis=0), 0.0)
+        out[pl.ds(half * 128, 128), :] = jnp.where(core == 0, value[:, :64], value[:, 64:]).astype(BF16)
     for copy in sent:
         copy.wait_send()
 
@@ -371,11 +388,11 @@
             b(4, 4, PZ, 128), b(4, 4, PX, 128), b(4, 4, PY, 128),
             b(3, 4, PZ, 128), b(3, 4, PX, 128), b(3, 4, PY, 128),
             b(4, PZ, 128), b(4, PX, 128), b(4, PY, 128),
-            b(3, PZ, 128), b(3, PX, 128), b(3, PY, 128),
-            b(128, 128), b(128, 128),
+            b(2, 3, PZ, 128), b(2, 3, PX, 128), b(2, 3, PY, 128),
+            b(PZ, 128), b(PX, 128), b(PY, 128),
             VMEM((8, 128), jnp.int32), SMEM((8, 128), jnp.int32),
             DMA((4,)), DMA((2, 6)), DMA((2, 4, 2)), DMA((2, 8, 2)), DMA((2, 8, 2)), DMA((2, 8)), DMA((2, 4)),
-            DMA((2, 3, 3, 4)), DMA((2, 3, 3)), DMA((2, 3, 3)), DMA((2,)),
+            DMA((2, 3, 3, 4)), DMA((2, 2, 3)), DMA((2, 3, 4)), DMA((3, 2, 3)), DMA((3, 2, 3)), DMA((2, 3)),
         ],
         compiler_params=pltpu.CompilerParams(
             collective_id=0, has_side_effects=True, vmem_limit_bytes=60 << 20

time: 69 us -> 54.8 us (0.79)
  Pallas kernels: 67.3 us -> 53 us
    pallas_call x1, Pallas kernels: 67.3 us -> 53 us  [local(): pl.pallas_call(kernel, name='sigma', out_shape=jax.ShapeDtypeStruct((256,...]
where the time goes in v3:
time: 54.8 us; the launch traced here: 54.6 us
  Pallas kernels  53 us (97%)
  local copies, waits for them, and re-layouts  1.54 us (3%)
    pallas_call x1, Pallas kernels, local(): pl.pallas_call(kernel, name='sigma', out_shape=jax.ShapeDtypeStruct((256,...  53 us
    pallas_call x1, local copies, waits for them, and re-layouts, local(): pl.pallas_call(kernel, name='sigma', out_shape=jax.ShapeDtypeStruct((256,...  1.54 us

profile of v3, /device:TPU:1, one launch (start us, length us, event | category | flops | bytes accessed | tf_op | source)
XLA Modules:
  0.0 54.6 jit_solution(4754988854423512268)
XLA Ops:
  0.0 53.0 %sigma.1 = bf16[256,64]{1,0:T(8,128)(2,1)} custom-call(s32[16]{0:T(128)} %partner.1, s32[16]{0:T(128)} %lens.1, s32[16,16]{1,0:T(8,128)} %targets.1, bf16[8,32,1024]{2,1,0:T(8,128)(2,1)} %bitcast.1, bf16[16,2,128,128]{3,2,1,0:T(8,128)(2,1)} %left.1, bf16[2,1024,1024]{2,1,0:T(8,128)(2,1)} %right.1), custom_call_target="tpu_custom_call" | custom-call | tf_op jit(solution)/shard_map/sigma/pallas_call | solution.py:377
  53.0 1.5 %copy.7 = bf16[256,64]{0,1:T(8,128)(2,1)} copy(bf16[256,64]{1,0:T(8,128)(2,1)} %sigma.1) | data formatting | bytes 65536 | tf_op jit(solution)/shard_map/sigma/pallas_call | solution.py:377

commit v4 on v3

--- a/solution.py
+++ b/solution.py
@@ -14,7 +14,8 @@
 
 
 def kernel(
-    partner, lens, targets, psi, left, right, out,
+    partner_in, lens_in, targets_in, psi, left, right, out,
+    partner, lens, targets,
     states, lsend, lrecv, lin, rops, image, runs, dsend, drecv,
     s1z, s1x, s1y, r1z, r1x, r1y, s2z, s2x, s2y, r2z, r2x, r2y, s3z, s3x, s3y, r3z, r3x, r3y,
     c3z, c3x, c3y,
@@ -53,10 +54,16 @@
         peers += [device(dc=c, **{axis: d}) for axis in ("dz", "dx", "dy") for c in range(2)] + [mate(d, 1)]
     for peer in peers:
         pl.semaphore_signal(barrier, inc=1, device_id=peer, device_id_type=MESH)
-    in_psi = pltpu.make_async_copy(psi, states.at[pl.ds(blk * 8, 8)], loc.at[0])
+    in_psi = pltpu.make_async_copy(psi, states.at[pl.ds(blk * 16, 16)], loc.at[0])
     in_left = pltpu.make_async_copy(left, lin, loc.at[1])
     in_right = pltpu.make_async_copy(right, rops, loc.at[2])
+    small = [
+        pltpu.make_async_copy(a, b, loc.at[4 + n])
+        for n, (a, b) in enumerate(((partner_in, partner), (lens_in, lens), (targets_in, targets)))
+    ]
     in_psi.start()
+    for copy in small:
+        copy.start()
     in_left.start()
     in_right.start()
 
@@ -64,7 +71,7 @@
 
     def unit(j, flip, parity, half, k, n=1):
         c = ((y + ys[j]) % 4) * 2 + (xl + flip) % 2
-        return states.at[pl.ds(((c * 2 + parity) * 2 + half) * 2 + k, n)]
+        return states.at[pl.ds(((c * 2 + parity) * 2 + half) * 4 + k, n)]
 
     mine = lambda j, flip, k, n=1: unit(j, flip, e, core, k, n)
 
@@ -72,15 +79,15 @@
         send(mine(j, 0, k), mine(j, 0, k), ysem.at[0, n], ysem.at[1, n], device(dy=dy))
 
     def x_out(j, k):
-        send(mine(j, 0, k), mine(j, 0, k), xsem.at[0, j, k], xsem.at[1, j, k], device(dx=1 if k == 0 else 3))
+        send(mine(j, 0, k), mine(j, 0, k), xsem.at[0, j, k], xsem.at[1, j, k], device(dx=1 if k < 2 else 3))
 
     def z_out(flip, j, k):
         n = flip * 4 + j
-        send(mine(j, flip, k), mine(j, flip, k), zsem.at[0, n, k], zsem.at[1, n, k], device(dz=1 if k == 0 else 3))
+        send(mine(j, flip, k), mine(j, flip, k), zsem.at[0, n, k], zsem.at[1, n, k], device(dz=1 if k < 2 else 3))
 
     def c_out(flip, j, other):
         n = flip * 4 + j
-        ref = unit(j, flip, (e + other) % 2, core, 0, 2)
+        ref = unit(j, flip, (e + other) % 2, core, 0, 4)
         send(ref, ref, csem.at[0, n, other], csem.at[1, n, other], device(dc=1))
 
     def l_out(dy, flip):
@@ -93,7 +100,7 @@
 
         @pl.loop(0, 2)
         def _(i):
-            rows = jnp.concatenate([states[pl.ds(q * 4, 4)].reshape(128, 1024) for q in at], axis=0)
+            rows = jnp.concatenate([states[pl.ds(q * 8, 8)].reshape(128, 1024) for q in at], axis=0)
             for n in range(4):
                 made = jnp.dot(rows, rops[i, :, n * 256 : n * 256 + 256], preferred_element_type=F32).astype(BF16)
                 for k in range(2):
@@ -101,9 +108,11 @@
 
     def images_of(*blocks):
         for flip, j, other in blocks:
-            arrived(unit(j, flip, (e + other) % 2, (core + 1) % 2, 0, 2), csem.at[1, flip * 4 + j, other])
+            arrived(unit(j, flip, (e + other) % 2, (core + 1) % 2, 0, 4), csem.at[1, flip * 4 + j, other])
         images(*blocks)
 
+    for copy in small:
+        copy.wait()
     number = lambda cond: jnp.where(cond, 1, 0)
     kk = lax.broadcasted_iota(jnp.int32, (32, 128), 0)
     lane = lax.broadcasted_iota(jnp.int32, (32, 128), 1)
@@ -134,12 +143,10 @@
 
     in_psi.wait()
     pl.semaphore_wait(barrier, len(peers))
-    y_out(0, 0, 0, 1)
-    y_out(1, 0, 1, 3)
-    x_out(0, 0)
-    x_out(0, 1)
-    y_out(2, 0, 1, 1)
-    y_out(3, 0, 0, 3)
+    for k in range(4):
+        y_out(k, 0, k, 1)
+        y_out(7 - k, 0, 3 - k, 3)
+        x_out(0, (0, 2, 1, 3)[k])
 
     in_left.wait()
     lane = lax.broadcasted_iota(jnp.int32, (128, 128), 1)
@@ -161,47 +168,57 @@
         x_out(j, k)
         z_out(0, j, k)
 
+    def near_y(k):
+        arrived(mine(1, 0, k), ysem.at[1, k])
+        if k < 2:
+            y_out(8 + k, 1, k, 1)
+        x_out(1, k)
+        z_out(0, 1, k)
+        m = 3 - k
+        arrived(mine(2, 0, m), ysem.at[1, 4 + m])
+        if m > 1:
+            y_out(8 + m, 2, m, 3)
+        x_out(2, m)
+        z_out(0, 2, m)
+
     def from_x(j, k):
         arrived(mine(j, 1, k), xsem.at[1, j, k])
         z_out(1, j, k)
 
     def from_z(flip, j):
-        for k in range(2):
+        for k in range(4):
             arrived(unit(j, flip, (e + 1) % 2, core, k), zsem.at[1, flip * 4 + j, k])
         c_out(flip, j, 1)
 
     images((0, 0, 0), (0, 0, 1))
-    from_y(1, 0, 0)
-    y_out(4, 1, 0, 1)
-    from_y(2, 1, 1)
-    y_out(5, 2, 1, 3)
-    from_x(0, 0)
-    from_x(0, 1)
+    near_y(0)
+    near_y(1)
+    for k in range(4):
+        from_x(0, k)
     c_out(1, 0, 0)
-    from_y(1, 1, 2)
+    near_y(2)
+    near_y(3)
     c_out(0, 1, 0)
-    from_y(2, 0, 3)
     c_out(0, 2, 0)
     l_out(1, 0)
     l_out(3, 0)
     l_out(2, 0)
-    images_of((1, 0, 0), (0, 1, 0))
-    from_y(3, 0, 4)
-    from_y(3, 1, 5)
+    for k in (0, 3, 1, 2):
+        from_y(3, k, 8 + k)
     c_out(0, 3, 0)
     for dy in (1, 3, 2):
         l_out(dy, 1)
-    from_x(1, 0)
-    from_x(2, 1)
-    from_x(1, 1)
+    images_of((1, 0, 0), (0, 1, 0))
+    for k in range(4):
+        from_x(1, k)
+        from_x(2, 3 - k)
     c_out(1, 1, 0)
-    from_x(2, 0)
     c_out(1, 2, 0)
     from_z(0, 1)
     from_z(0, 2)
     images_of((0, 2, 0), (0, 3, 0))
-    from_x(3, 0)
-    from_x(3, 1)
+    for k in (0, 3, 1, 2):
+        from_x(3, k)
     c_out(1, 3, 0)
     from_z(1, 0)
     images_of((0, 1, 1), (0, 2, 1))
@@ -365,23 +382,24 @@
         own = (c3z[...], c3x[...], c3y[...]) if other else (s3z[y], s3x[3], s3y[x])
         parts = [summed(a, [got[half, d] for d in range(3)]) for a, got in zip(own, (r3z, r3x, r3y))]
         value = jnp.where(row < lens[2 * blk + half], jnp.concatenate(parts, axis=0), 0.0)
-        out[pl.ds(half * 128, 128), :] = jnp.where(core == 0, value[:, :64], value[:, 64:]).astype(BF16)
+        turned = value.T
+        out[:, pl.ds(pl.multiple_of(half * 128, 128), 128)] = jnp.where(core == 0, turned[:64], turned[64:]).astype(BF16)
     for copy in sent:
         copy.wait_send()
 
 
 def local(psi, left_blocks, right_ops, block_target, left_partner, block_len):
-    smem = pl.BlockSpec(memory_space=SMEM)
     hbm = pl.BlockSpec(memory_space=pl.ANY)
     b = lambda *shape: VMEM(shape, BF16)
     return pl.pallas_call(
         kernel,
         name="sigma",
-        out_shape=jax.ShapeDtypeStruct((256, 64), BF16),
-        in_specs=[smem, smem, smem, hbm, hbm, hbm],
+        out_shape=jax.ShapeDtypeStruct((64, 256), BF16),
+        in_specs=[hbm] * 6,
         out_specs=pl.BlockSpec(memory_space=VMEM),
         scratch_shapes=[
-            b(64, 32, 1024), b(8, 4, 128, 128), b(8, 4, 128, 128), b(16, 2, 128, 128), b(2, 1024, 1024),
+            SMEM((16,), jnp.int32), SMEM((16,), jnp.int32), SMEM((16, 16), jnp.int32),
+            b(128, 16, 1024), b(8, 4, 128, 128), b(8, 4, 128, 128), b(16, 2, 128, 128), b(2, 1024, 1024),
             b(4, 32, 128, 256), b(2, 32, 128, 256), b(4, 8, 128, 256), b(4, 8, 128, 256),
             b(4, 16, PZ, 128), b(4, 4, 4, PX, 128), b(4, 4, 4, PY, 128),
             b(3, 16, PZ, 128), b(3, 4, 4, PX, 128), b(3, 4, 4, PY, 128),
@@ -391,13 +409,13 @@
             b(2, 3, PZ, 128), b(2, 3, PX, 128), b(2, 3, PY, 128),
             b(PZ, 128), b(PX, 128), b(PY, 128),
             VMEM((8, 128), jnp.int32), SMEM((8, 128), jnp.int32),
-            DMA((4,)), DMA((2, 6)), DMA((2, 4, 2)), DMA((2, 8, 2)), DMA((2, 8, 2)), DMA((2, 8)), DMA((2, 4)),
+            DMA((7,)), DMA((2, 12)), DMA((2, 4, 4)), DMA((2, 8, 4)), DMA((2, 8, 2)), DMA((2, 8)), DMA((2, 4)),
             DMA((2, 3, 3, 4)), DMA((2, 2, 3)), DMA((2, 3, 4)), DMA((3, 2, 3)), DMA((3, 2, 3)), DMA((2, 3)),
         ],
         compiler_params=pltpu.CompilerParams(
             collective_id=0, has_side_effects=True, vmem_limit_bytes=60 << 20
         ),
-    )(left_partner, block_len, block_target, psi.reshape(8, 32, 1024), left_blocks, right_ops)
+    )(left_partner, block_len, block_target, psi.reshape(16, 16, 1024), left_blocks, right_ops).T
 
 
 def solution(mesh):

time: 54.8 us -> 52.8 us (0.964)
  Pallas kernels: 53 us -> 51.2 us
    pallas_call x1, Pallas kernels: 53 us -> 51.2 us  [local(): pl.pallas_call(kernel, name='sigma', out_shape=jax.ShapeDtypeStruct((64,...]
    pallas_call x1 -> x0, local copies, waits for them, and re-layouts: 1.54 us -> none  [local(): pl.pallas_call(kernel, name='sigma', out_shape=jax.ShapeDtypeStruct((256,...]
    unnamed x0 -> x1, local copies, waits for them, and re-layouts: none -> 1.38 us
where the time goes in v4:
time: 52.8 us; the launch traced here: 52.6 us
  Pallas kernels  51.2 us (97%)
  local copies, waits for them, and re-layouts  1.38 us (3%)
    pallas_call x1, Pallas kernels, local(): pl.pallas_call(kernel, name='sigma', out_shape=jax.ShapeDtypeStruct((64,...  51.2 us
    unnamed x1, local copies, waits for them, and re-layouts  1.38 us

profile of v4, /device:TPU:1, one launch (start us, length us, event | category | flops | bytes accessed | tf_op | source)
XLA Modules:
  0.0 52.6 jit_solution(17868673449850069526)
XLA Ops:
  0.0 51.2 %sigma.1 = bf16[64,256]{1,0:T(8,128)(2,1)} custom-call(s32[16]{0:T(128)} %partner_in.1, s32[16]{0:T(128)} %lens_in.1, s32[16,16]{1,0:T(8,128)} %targets_in.1, bf16[16,16,1024]{2,1,0:T(8,128)(2,1)} %bitcast.2, bf16[16,2,128,128]{3,2,1,0:T(8,128)(2,1)} %left.1, bf16[2,1024,1024]{2,1,0:T(8,128)(2,1)} %right.1), custom_call_target="tpu_custom_call" | custom-call | tf_op jit(solution)/shard_map/sigma/pallas_call | solution.py:394
  51.2 1.4 %copy.8 = bf16[256,64]{0,1:T(8,128)(2,1)} copy(bf16[256,64]{0,1:T(8,128)(2,1)} %bitcast.3) | data formatting | bytes 65536

commit v5 on v4

--- a/solution.py
+++ b/solution.py
@@ -78,12 +78,23 @@
     def y_out(n, j, k, dy):
         send(mine(j, 0, k), mine(j, 0, k), ysem.at[0, n], ysem.at[1, n], device(dy=dy))
 
+    ready = set()
+
     def x_out(j, k):
-        send(mine(j, 0, k), mine(j, 0, k), xsem.at[0, j, k], xsem.at[1, j, k], device(dx=1 if k < 2 else 3))
+        half = k // 2
+        ready.add((j, k))
+        if (j, k ^ 1) in ready:
+            ref = mine(j, 0, half * 2, 2)
+            send(ref, ref, xsem.at[0, j, half], xsem.at[1, j, half], device(dx=3 if half else 1))
+
+    seen = set()
 
     def z_out(flip, j, k):
-        n = flip * 4 + j
-        send(mine(j, flip, k), mine(j, flip, k), zsem.at[0, n, k], zsem.at[1, n, k], device(dz=1 if k < 2 else 3))
+        n, half = flip * 4 + j, k // 2
+        seen.add((n, k))
+        if (n, k ^ 1) in seen:
+            ref = mine(j, flip, half * 2, 2)
+            send(ref, ref, zsem.at[0, n, half], zsem.at[1, n, half], device(dz=3 if half else 1))
 
     def c_out(flip, j, other):
         n = flip * 4 + j
@@ -182,12 +193,14 @@
         z_out(0, 2, m)
 
     def from_x(j, k):
-        arrived(mine(j, 1, k), xsem.at[1, j, k])
-        z_out(1, j, k)
+        if k % 2 == 0:
+            arrived(mine(j, 1, k, 2), xsem.at[1, j, k // 2])
+            z_out(1, j, k)
+            z_out(1, j, k + 1)
 
     def from_z(flip, j):
-        for k in range(4):
-            arrived(unit(j, flip, (e + 1) % 2, core, k), zsem.at[1, flip * 4 + j, k])
+        for k in range(2):
+            arrived(unit(j, flip, (e + 1) % 2, core, 2 * k, 2), zsem.at[1, flip * 4 + j, k])
         c_out(flip, j, 1)
 
     images((0, 0, 0), (0, 0, 1))
@@ -257,18 +270,17 @@
         return value * table[4, t].astype(F32)
 
     def swap(zi):
-        @pl.loop(0, 8)
-        def _(c):
-            dsend[zi, c] = total(zi, 2 * c + 1 - core).astype(BF16)
-
-    def swap_out(zi):
-        send(dsend.at[zi], drecv.at[zi], dsem.at[0, zi], dsem.at[1, zi], device(dc=1))
+        for half in range(2):
+
+            @pl.loop(half * 4, half * 4 + 4, unroll=True)
+            def _(c):
+                dsend[zi, c] = total(zi, 2 * c + 1 - core).astype(BF16)
+
+            part = pl.ds(half * 4, 4)
+            send(dsend.at[zi, part], drecv.at[zi, part], dsem.at[0, zi, half], dsem.at[1, zi, half], device(dc=1))
 
     def join(zi):
-        arrived(drecv.at[zi], dsem.at[1, zi])
-
-        @pl.loop(0, 4)
-        def _(yd):
+        def rows_of(yd):
             for xld in range(2):
                 c = yd * 2 + xld
                 value = (total(zi, 2 * c + core) + drecv[zi, c].astype(F32)).astype(BF16)
@@ -278,6 +290,10 @@
                     s1x[xhd * 2 + xld, zi, yd] = part[PZ : PZ + PX]
                     s1y[yd, zi, xhd * 2 + xld] = part[PZ + PX :]
 
+        for half in range(2):
+            arrived(drecv.at[zi, pl.ds(half * 4, 4)], dsem.at[1, zi, half])
+            pl.loop(half * 2, half * 2 + 2, unroll=True)(rows_of)
+
     def first_out(zi):
         for d in (1, 2, 3):
             send(s1x.at[(x + d) % 4, zi], r1x.at[d - 1, zi], sem1.at[0, 1, d - 1, zi], sem1.at[1, 1, d - 1, zi], device(dx=d))
@@ -288,7 +304,6 @@
     for zi in range(4):
         mix(zi)
         swap(zi)
-        swap_out(zi)
         if zi >= 1:
             join(zi - 1)
             first_out(zi - 1)
@@ -409,7 +424,7 @@
             b(2, 3, PZ, 128), b(2, 3, PX, 128), b(2, 3, PY, 128),
             b(PZ, 128), b(PX, 128), b(PY, 128),
             VMEM((8, 128), jnp.int32), SMEM((8, 128), jnp.int32),
-            DMA((7,)), DMA((2, 12)), DMA((2, 4, 4)), DMA((2, 8, 4)), DMA((2, 8, 2)), DMA((2, 8)), DMA((2, 4)),
+            DMA((7,)), DMA((2, 12)), DMA((2, 4, 2)), DMA((2, 8, 2)), DMA((2, 8, 2)), DMA((2, 8)), DMA((2, 4, 2)),
             DMA((2, 3, 3, 4)), DMA((2, 2, 3)), DMA((2, 3, 4)), DMA((3, 2, 3)), DMA((3, 2, 3)), DMA((2, 3)),
         ],
         compiler_params=pltpu.CompilerParams(

time: 52.8 us -> 52.1 us (0.987)
  Pallas kernels: 51.2 us -> 50.6 us
    pallas_call x1, Pallas kernels: 51.2 us -> 50.6 us  [local(): pl.pallas_call(kernel, name='sigma', out_shape=jax.ShapeDtypeStruct((64,...]
where the time goes in v5:
time: 52.1 us; the launch traced here: 52 us
  Pallas kernels  50.6 us (97%)
  local copies, waits for them, and re-layouts  1.38 us (3%)
    pallas_call x1, Pallas kernels, local(): pl.pallas_call(kernel, name='sigma', out_shape=jax.ShapeDtypeStruct((64,...  50.6 us
    unnamed x1, local copies, waits for them, and re-layouts  1.38 us

profile of v5, /device:TPU:1, one launch (start us, length us, event | category | flops | bytes accessed | tf_op | source)
XLA Modules:
  0.0 52.0 jit_solution(9708637073845042788)
XLA Ops:
  0.0 50.6 %sigma.1 = bf16[64,256]{1,0:T(8,128)(2,1)} custom-call(s32[16]{0:T(128)} %partner_in.1, s32[16]{0:T(128)} %lens_in.1, s32[16,16]{1,0:T(8,128)} %targets_in.1, bf16[16,16,1024]{2,1,0:T(8,128)(2,1)} %bitcast.2, bf16[16,2,128,128]{3,2,1,0:T(8,128)(2,1)} %left.1, bf16[2,1024,1024]{2,1,0:T(8,128)(2,1)} %right.1), custom_call_target="tpu_custom_call" | custom-call | tf_op jit(solution)/shard_map/sigma/pallas_call | solution.py:409
  50.6 1.4 %copy.8 = bf16[256,64]{0,1:T(8,128)(2,1)} copy(bf16[256,64]{0,1:T(8,128)(2,1)} %bitcast.3) | data formatting | bytes 65536

commit v6 on v5

--- a/solution.py
+++ b/solution.py
@@ -274,7 +274,9 @@
 
             @pl.loop(half * 4, half * 4 + 4, unroll=True)
             def _(c):
-                dsend[zi, c] = total(zi, 2 * c + 1 - core).astype(BF16)
+                t = 2 * c + 1 - core
+                value = runs[zi % 2, table[3, t]]
+                dsend[zi, c] = jnp.where(table[4, t] > 0, value, jnp.zeros_like(value))
 
             part = pl.ds(half * 4, 4)
             send(dsend.at[zi, part], drecv.at[zi, part], dsem.at[0, zi, half], dsem.at[1, zi, half], device(dc=1))

time: 52.1 us -> 52.1 us (level)
  no operation moved by 1% of the time
where the time goes in v6:
time: 52.1 us; the launch traced here: 51.9 us
  Pallas kernels  50.6 us (97%)
  local copies, waits for them, and re-layouts  1.38 us (3%)
    pallas_call x1, Pallas kernels, local(): pl.pallas_call(kernel, name='sigma', out_shape=jax.ShapeDtypeStruct((64,...  50.6 us
    unnamed x1, local copies, waits for them, and re-layouts  1.38 us

profile of v6, /device:TPU:1, one launch (start us, length us, event | category | flops | bytes accessed | tf_op | source)
XLA Modules:
  0.0 51.9 jit_solution(4189350267640623076)
XLA Ops:
  0.0 50.6 %sigma.1 = bf16[64,256]{1,0:T(8,128)(2,1)} custom-call(s32[16]{0:T(128)} %partner_in.1, s32[16]{0:T(128)} %lens_in.1, s32[16,16]{1,0:T(8,128)} %targets_in.1, bf16[16,16,1024]{2,1,0:T(8,128)(2,1)} %bitcast.2, bf16[16,2,128,128]{3,2,1,0:T(8,128)(2,1)} %left.1, bf16[2,1024,1024]{2,1,0:T(8,128)(2,1)} %right.1), custom_call_target="tpu_custom_call" | custom-call | tf_op jit(solution)/shard_map/sigma/pallas_call | solution.py:411
  50.6 1.4 %copy.8 = bf16[256,64]{0,1:T(8,128)(2,1)} copy(bf16[256,64]{0,1:T(8,128)(2,1)} %bitcast.3) | data formatting | bytes 65536
